TPU v7x, 32 devices: a whole 2x2x4 slice. The times are simulated.
32 devices in a mesh: blk: 16 (over z, y, x), ch: 2 (over core).
Axes of the slice: x: 2, y: 2, z: 4, core: 2. Of those that a mesh axis runs over, the one named last changes fastest.
Arguments:
- features: bfloat16 [4096, 128], P('blk'), may hold values from -6 to 6
- out_grad: bfloat16 [4096, 256], P('blk', 'ch'), may hold values from -6 to 6
- weight: bfloat16 [256, 256], P('ch'), may hold values from -0.375 to 0.375
- neighbour_slot: int32 [4096, 20], P('blk'), may hold values from 0 to 2303
- argmax_edge: int32 [4096, 256], P('blk', 'ch'), may hold values from 0 to 19
Outputs:
- feature_grad: float32 [4096, 128], P('blk')
- weight_grad: float32 [256, 256], P('ch')
Inputs may be any that keep to these rules, and one draw needn't show every extreme that they name: `neighbour_slot`: slot s stands for row s mod 256 of the block s // 256 - 4 places away from the point's own block around the cycle.
All inputs are finite; a program needn't handle non-finite values.
Results may differ from a plain program's by a relative error of at most 0.0044.
Values may be sent and summed in bfloat16 or wider, within the bound.
No kernel may reach another device: no remote copies, remote signals or barrier semaphores. Data moves between devices by JAX's collectives and lax.ppermute only.
A program may use at most 64 MiB of HBM per device.

v0:
```python
import jax
import jax.numpy as jnp
from jax import lax
from jax.sharding import PartitionSpec as P

REACH = 4


def shifted(block, axis, distance):
    devices = range(lax.axis_size(axis))
    route = [((i - distance) % len(devices), i) for i in devices]
    return lax.ppermute(block, axis, route)


def silu_slope(pre):
    sig = jax.nn.sigmoid(pre)
    return sig * (1.0 + pre * (1.0 - sig))


def fetch_blocks(piece):
    fetched = []
    for offset in range(-REACH, REACH + 1):
        if offset != 0:
            fetched.append(shifted(piece, "blk", -offset))
    return fetched


def deliver_blocks(stacked):
    summed_all = stacked[REACH]
    for position in range(2 * REACH + 1):
        if position != REACH:
            summed_all = summed_all + shifted(stacked[position], "blk", position - REACH)
    return summed_all


def on_device(features, out_grad, weight, neighbour_slot, argmax_edge):
    points = features.shape[0]
    in_width = features.shape[1]
    columns = weight.shape[0]
    neighbours = neighbour_slot.shape[1]
    w_self = weight[:, :in_width]
    w_nbr = weight[:, in_width:]
    w_diff = (w_self.astype(jnp.float32) - w_nbr.astype(jnp.float32)).astype(jnp.bfloat16)
    remote_list = fetch_blocks(features)
    window = jnp.concatenate(remote_list[:REACH] + [features] + remote_list[REACH:], axis=0)
    window_rows = window.shape[0]
    self_term = jnp.dot(features, w_diff.T, preferred_element_type=jnp.float32)
    w_nbr_t = w_nbr.T
    block_rows = min(256, points)
    block_count = points // block_rows
    window_ids = jnp.arange(window_rows, dtype=jnp.int32)
    edge_order = jnp.arange(neighbours, dtype=jnp.int32)

    def point_block(window_acc, inputs):
        self_rows, slot_rows, grad_rows, pick_rows = inputs
        grad_float = grad_rows.astype(jnp.float32)

        def per_edge(carry, edge_index):
            acc_window, edge_total = carry
            slot_col = lax.dynamic_slice_in_dim(slot_rows, edge_index, 1, 1)
            one_hot = (slot_col == window_ids[None, :]).astype(jnp.bfloat16)
            picked = jnp.dot(one_hot, window, preferred_element_type=jnp.float32).astype(
                jnp.bfloat16
            )
            pre = self_rows + jnp.dot(picked, w_nbr_t, preferred_element_type=jnp.float32)
            keep = pick_rows == edge_index
            edge_grad = jnp.where(keep, grad_float * silu_slope(pre), 0.0).astype(jnp.bfloat16)
            edge_total = edge_total + edge_grad.astype(jnp.float32)
            acc_window = acc_window + lax.dot_general(
                one_hot, edge_grad, (((0,), (0,)), ((), ())), preferred_element_type=jnp.float32
            )
            return ((acc_window, edge_total), None)

        start_total = jnp.zeros((self_rows.shape[0], columns), jnp.float32)
        (window_acc, edge_total), _ = lax.scan(per_edge, (window_acc, start_total), edge_order)
        return (window_acc, edge_total.astype(jnp.bfloat16))

    start_window = jnp.zeros((window_rows, columns), jnp.float32)
    gathered_float, grad_sum = lax.scan(
        point_block,
        start_window,
        (
            self_term.reshape(block_count, block_rows, columns),
            neighbour_slot.reshape(block_count, block_rows, neighbours),
            out_grad.reshape(block_count, block_rows, columns),
            argmax_edge.reshape(block_count, block_rows, columns),
        ),
    )
    gathered = gathered_float.astype(jnp.bfloat16)
    grad_sum = grad_sum.reshape(points, columns)
    own_part = lax.dot_general(
        grad_sum, features, (((0,), (0,)), ((), ())), preferred_element_type=jnp.float32
    )
    nbr_total = lax.dot_general(
        gathered, window, (((0,), (0,)), ((), ())), preferred_element_type=jnp.float32
    )
    weight_terms = jnp.concatenate([own_part, nbr_total - own_part], axis=1)
    total_points = points * lax.axis_size("blk")
    weight_grad = lax.psum(weight_terms, "blk") * total_points ** (-0.5)
    self_grad = jnp.dot(grad_sum, w_diff, preferred_element_type=jnp.float32)
    contrib = jnp.dot(gathered, w_nbr, preferred_element_type=jnp.float32)
    contrib = contrib.reshape(2 * REACH + 1, points, in_width)
    contrib = contrib.at[REACH].add(self_grad)
    summed = deliver_blocks(contrib)
    feature_grad = lax.psum(summed, "ch")
    return (feature_grad, weight_grad)


def solution(mesh):
    return jax.shard_map(
        on_device,
        mesh=mesh,
        in_specs=(P("blk", None), P("blk", "ch"), P("ch", None), P("blk", None), P("blk", "ch")),
        out_specs=(P("blk", None), P("ch", None)),
        check_vma=False,
    )
```

profile of v0, /device:TPU:0, one launch (start us, length us, event | category | flops | bytes accessed | tf_op | source)
XLA Modules:
  0.0 308.4 jit_solution(1734680084352292004)
XLA Ops:
  7.2 5.1 %collective-permute-start.7 = (bf16[256,128]{1,0:T(8,128)(2,1)}, bf16[256,128]{1,0:T(8,128)(2,1)S(1)}, u32[]{:S(2)}, u32[]{:S(2)}) collective-permute-start(bf16[256,128]{1,0:T(8,128)(2,1)} %param.9), channel_id=1, source_target_pairs={{8,0},{10,2},{12,4},{14,6},{16,8},{18,10},{20,12},{22,14},{24,16},... | collective-permute-start | bytes 196616 | tf_op jit(solution)/shard_map/ppermute | solution.py:12
  12.4 1.4 collective-permute-start.6
  13.7 1.4 collective-permute-start.5
  15.1 1.4 collective-permute-start.4
  16.6 1.6 collective-permute-start
  21.2 1.7 collective-permute-done
  23.5 6.5 %collective-permute-done.1 = bf16[256,128]{1,0:T(8,128)(2,1)S(1)} collective-permute-done((bf16[256,128]{1,0:T(8,128)(2,1)}, bf16[256,128]{1,0:T(8,128)(2,1)S(1)}, u32[]{:S(2)}, u32[]{:S(2)}) %collective-permute-start.1) | collective-permute-done | bytes 65568 | tf_op jit(solution)/shard_map/ppermute | solution.py:12
  30.7 6.5 %collective-permute-done.2 = bf16[256,128]{1,0:T(8,128)(2,1)S(1)} collective-permute-done((bf16[256,128]{1,0:T(8,128)(2,1)}, bf16[256,128]{1,0:T(8,128)(2,1)S(1)}, u32[]{:S(2)}, u32[]{:S(2)}) %collective-permute-start.2) | collective-permute-done | bytes 65568 | tf_op jit(solution)/shard_map/ppermute | solution.py:12
  37.2 1.5 collective-permute-start.3
  38.7 6.4 %collective-permute-done.3 = bf16[256,128]{1,0:T(8,128)(2,1)S(1)} collective-permute-done((bf16[256,128]{1,0:T(8,128)(2,1)S(1)}, bf16[256,128]{1,0:T(8,128)(2,1)S(1)}, u32[]{:S(2)}, u32[]{:S(2)}) %collective-permute-start.3) | collective-permute-done | bytes 65568 | tf_op jit(solution)/shard_map/ppermute | solution.py:12
  45.2 117.4 %while.23 = (s32[]{:T(128)}, f32[2304,128]{1,0:T(8,128)S(1)}, f32[256,128]{1,0:T(8,128)S(1)}, s32[20]{0:T(128)S(1)}, s32[256,20]{0,1:T(8,128)}, /*index=5*/s32[2...) while((s32[]{:T(128)}, f32[2304,128]{1,0:T(8,128)S(1)}, ...), condition=%wide.region_1.2_spmd.clone, body=%wide.region_0.1_spmd.clone.sunk | while | flops 312672256 | bytes 3772614 | solution.py:75
  48.5 1.3 select_add_fusion.2
  54.4 1.3 select_add_fusion.2
  60.2 1.3 select_add_fusion.2
  66.1 1.3 select_add_fusion.2
  72.0 1.3 select_add_fusion.2
  77.8 1.3 select_add_fusion.2
  83.7 1.3 select_add_fusion.2
  89.6 1.3 select_add_fusion.2
  95.5 1.3 select_add_fusion.2
  148.3 1.3 select_add_fusion.2
  163.8 2.0 collective-permute-start.15
  165.8 1.5 collective-permute-start.12
  167.5 1.6 collective-permute-done.8
  169.1 2.6 collective-permute-start.11
  172.0 1.8 collective-permute-start.10
  174.5 2.0 collective-permute-start.9
  177.6 3.0 collective-permute-done.9
  180.6 2.1 fusion.13
  182.7 97.4 %all-reduce.5.cloned.1.call-done = f32[128,256]{0,1:T(8,128)} async-done(((f32[128,256]{0,1:T(8,128)}), f32[128,256]{0,1:T(8,128)}) %all-reduce.5.cloned.1.call-update) | async-done | bytes 131088 | tf_op jit(solution)/shard_map/psum | solution.py:99
  281.8 18.2 %all-reduce.3.cloned.1.call-done = f32[256,128]{1,0:T(8,128)} async-done(((f32[256,128]{1,0:T(8,128)}), f32[256,128]{1,0:T(8,128)}) %all-reduce.3.cloned.1.call-update) | async-done | bytes 131088 | tf_op jit(solution)/shard_map/psum | solution.py:105
  299.9 1.6 copy.32
  (122 shorter events, 74.2 us)
Async XLA Ops:
  7.2 30.0 %copy-start = (bf16[256,128]{1,0:T(8,128)(2,1)S(1)}, bf16[256,128]{1,0:T(8,128)(2,1)}, u32[]{:S(2)}) copy-start(bf16[256,128]{1,0:T(8,128)(2,1)} %param.9) | copy-start | bytes 196612
  7.2 38.1 %copy-start.3 = (s32[256,128]{1,0:T(8,128)S(1)}, s32[256,128]{1,0:T(8,128)}, u32[]{:S(2)}) copy-start(s32[256,128]{1,0:T(8,128)} %param.13) | copy-start | bytes 393220
  7.2 272.9 %all-reduce.5.cloned.1.call-start = ((), (), s32[]{:S(2)}) async-start(), calls=%async_computation.1 | async-start | bytes 262144 | tf_op jit(solution)/shard_map/psum | solution.py:99
  7.2 38.0 %collective-permute-start.7 = (bf16[256,128]{1,0:T(8,128)(2,1)}, bf16[256,128]{1,0:T(8,128)(2,1)S(1)}, u32[]{:S(2)}, u32[]{:S(2)}) collective-permute-start(bf16[256,128]{1,0:T(8,128)(2,1)} %param.9), channel_id=1, source_target_pairs={{8,0},{10,2},{12,4},{14,6},{16,8},{18,10},{20,12},{22,14},{24,16},... | collective-permute-start | bytes 196616 | tf_op jit(solution)/shard_map/ppermute | solution.py:12
  12.4 32.8 %collective-permute-start.6 = (bf16[256,128]{1,0:T(8,128)(2,1)}, bf16[256,128]{1,0:T(8,128)(2,1)S(1)}, u32[]{:S(2)}, u32[]{:S(2)}) collective-permute-start(bf16[256,128]{1,0:T(8,128)(2,1)} %param.9), channel_id=1, source_target_pairs={{6,0},{8,2},{10,4},{12,6},{14,8},{16,10},{18,12},{20,14},{22,16},{... | collective-permute-start | bytes 196616 | tf_op jit(solution)/shard_map/ppermute | solution.py:12
  13.7 31.4 %collective-permute-start.5 = (bf16[256,128]{1,0:T(8,128)(2,1)}, bf16[256,128]{1,0:T(8,128)(2,1)S(1)}, u32[]{:S(2)}, u32[]{:S(2)}) collective-permute-start(bf16[256,128]{1,0:T(8,128)(2,1)} %param.9), channel_id=1, source_target_pairs={{4,0},{6,2},{8,4},{10,6},{12,8},{14,10},{16,12},{18,14},{20,16},{2... | collective-permute-start | bytes 196616 | tf_op jit(solution)/shard_map/ppermute | solution.py:12
  15.1 30.0 %collective-permute-start.4 = (bf16[256,128]{1,0:T(8,128)(2,1)}, bf16[256,128]{1,0:T(8,128)(2,1)S(1)}, u32[]{:S(2)}, u32[]{:S(2)}) collective-permute-start(bf16[256,128]{1,0:T(8,128)(2,1)} %param.9), channel_id=1, source_target_pairs={{2,0},{4,2},{6,4},{8,6},{10,8},{12,10},{14,12},{16,14},{18,16},{20... | collective-permute-start | bytes 196616 | tf_op jit(solution)/shard_map/ppermute | solution.py:12
  16.6 6.3 %collective-permute-start = (bf16[256,128]{1,0:T(8,128)(2,1)}, bf16[256,128]{1,0:T(8,128)(2,1)S(1)}, u32[]{:S(2)}, u32[]{:S(2)}) collective-permute-start(bf16[256,128]{1,0:T(8,128)(2,1)} %param.9), channel_id=1, source_target_pairs={{24,0},{26,2},{28,4},{30,6},{0,8},{2,10},{4,12},{6,14},{8,16},{10,... | collective-permute-start | bytes 196616 | tf_op jit(solution)/shard_map/ppermute | solution.py:12
  22.9 7.2 %collective-permute-start.1 = (bf16[256,128]{1,0:T(8,128)(2,1)}, bf16[256,128]{1,0:T(8,128)(2,1)S(1)}, u32[]{:S(2)}, u32[]{:S(2)}) collective-permute-start(bf16[256,128]{1,0:T(8,128)(2,1)} %param.9), channel_id=1, source_target_pairs={{26,0},{28,2},{30,4},{0,6},{2,8},{4,10},{6,12},{8,14},{10,16},{12,... | collective-permute-start | bytes 196616 | tf_op jit(solution)/shard_map/ppermute | solution.py:12
  30.0 7.2 %collective-permute-start.2 = (bf16[256,128]{1,0:T(8,128)(2,1)}, bf16[256,128]{1,0:T(8,128)(2,1)S(1)}, u32[]{:S(2)}, u32[]{:S(2)}) collective-permute-start(bf16[256,128]{1,0:T(8,128)(2,1)} %param.9), channel_id=1, source_target_pairs={{28,0},{30,2},{0,4},{2,6},{4,8},{6,10},{8,12},{10,14},{12,16},{14,... | collective-permute-start | bytes 196616 | tf_op jit(solution)/shard_map/ppermute | solution.py:12
  37.2 7.9 %collective-permute-start.3 = (bf16[256,128]{1,0:T(8,128)(2,1)S(1)}, bf16[256,128]{1,0:T(8,128)(2,1)S(1)}, u32[]{:S(2)}, u32[]{:S(2)}) collective-permute-start(bf16[256,128]{1,0:T(8,128)(2,1)S(1)} %copy-done), channel_id=1, source_target_pairs={{30,0},{0,2},{2,4},{4,6},{6,8},{8,10},{10,12},{12,14},{14,16},{16,... | collective-permute-start | bytes 196616 | tf_op jit(solution)/shard_map/ppermute | solution.py:12
  45.2 117.4 %copy-start.1 = (bf16[128,256]{1,0:T(8,128)(2,1)S(1)}, bf16[128,256]{1,0:T(8,128)(2,1)}, u32[]{:S(2)}) copy-start(bf16[128,256]{1,0:T(8,128)(2,1)} %param.11) | copy-start | bytes 196612
  163.8 5.3 %collective-permute-start.8 = (f32[256,128]{1,0:T(8,128)S(1)}, f32[256,128]{1,0:T(8,128)S(1)}, u32[]{:S(2)}, u32[]{:S(2)}) collective-permute-start(f32[256,128]{1,0:T(8,128)S(1)} %get-tuple-element.176), channel_id=1, source_target_pairs={{8,0},{10,2},{12,4},{14,6},{16,8},{18,10},{20,12},{22,14},{24,16},... | collective-permute-start | bytes 393224 | tf_op jit(solution)/shard_map/ppermute | solution.py:12
  163.8 8.2 %collective-permute-start.15 = (f32[256,128]{1,0:T(8,128)S(1)}, f32[256,128]{1,0:T(8,128)S(1)}, u32[]{:S(2)}, u32[]{:S(2)}) collective-permute-start(f32[256,128]{1,0:T(8,128)S(1)} %get-tuple-element.177), channel_id=1, source_target_pairs={{24,0},{26,2},{28,4},{30,6},{0,8},{2,10},{4,12},{6,14},{8,16},{10,... | collective-permute-start | bytes 393224 | tf_op jit(solution)/shard_map/ppermute | solution.py:12
  165.8 8.0 %collective-permute-start.14 = (f32[256,128]{1,0:T(8,128)S(1)}, f32[256,128]{1,0:T(8,128)S(1)}, u32[]{:S(2)}, u32[]{:S(2)}) collective-permute-start(f32[256,128]{1,0:T(8,128)S(1)} %get-tuple-element.178), channel_id=1, source_target_pairs={{26,0},{28,2},{30,4},{0,6},{2,8},{4,10},{6,12},{8,14},{10,16},{12,... | collective-permute-start | bytes 393224 | tf_op jit(solution)/shard_map/ppermute | solution.py:12
  165.8 11.7 %collective-permute-start.13 = (f32[256,128]{1,0:T(8,128)}, f32[256,128]{1,0:T(8,128)}, u32[]{:S(2)}, u32[]{:S(2)}) collective-permute-start(f32[256,128]{1,0:T(8,128)} %get-tuple-element.179), channel_id=1, source_target_pairs={{28,0},{30,2},{0,4},{2,6},{4,8},{6,10},{8,12},{10,14},{12,16},{14,... | collective-permute-start | bytes 393224 | tf_op jit(solution)/shard_map/ppermute | solution.py:12
  165.8 11.7 %collective-permute-start.12 = (f32[256,128]{1,0:T(8,128)}, f32[256,128]{1,0:T(8,128)}, u32[]{:S(2)}, u32[]{:S(2)}) collective-permute-start(f32[256,128]{1,0:T(8,128)} %get-tuple-element.180), channel_id=1, source_target_pairs={{30,0},{0,2},{2,4},{4,6},{6,8},{8,10},{10,12},{12,14},{14,16},{16,... | collective-permute-start | bytes 393224 | tf_op jit(solution)/shard_map/ppermute | solution.py:12
  169.1 8.4 %collective-permute-start.11 = (f32[256,128]{1,0:T(8,128)}, f32[256,128]{1,0:T(8,128)}, u32[]{:S(2)}, u32[]{:S(2)}) collective-permute-start(f32[256,128]{1,0:T(8,128)} %get-tuple-element.181), channel_id=1, source_target_pairs={{2,0},{4,2},{6,4},{8,6},{10,8},{12,10},{14,12},{16,14},{18,16},{20... | collective-permute-start | bytes 393224 | tf_op jit(solution)/shard_map/ppermute | solution.py:12
  172.0 5.6 %collective-permute-start.10 = (f32[256,128]{1,0:T(8,128)}, f32[256,128]{1,0:T(8,128)}, u32[]{:S(2)}, u32[]{:S(2)}) collective-permute-start(f32[256,128]{1,0:T(8,128)} %get-tuple-element.182), channel_id=1, source_target_pairs={{4,0},{6,2},{8,4},{10,6},{12,8},{14,10},{16,12},{18,14},{20,16},{2... | collective-permute-start | bytes 393224 | tf_op jit(solution)/shard_map/ppermute | solution.py:12
  173.8 0.7 copy-start.2
  174.5 6.2 %collective-permute-start.9 = (f32[256,128]{1,0:T(8,128)}, f32[256,128]{1,0:T(8,128)}, u32[]{:S(2)}, u32[]{:S(2)}) collective-permute-start(f32[256,128]{1,0:T(8,128)} %get-tuple-element.183), channel_id=1, source_target_pairs={{6,0},{8,2},{10,4},{12,6},{14,8},{16,10},{18,12},{20,14},{22,16},{... | collective-permute-start | bytes 393224 | tf_op jit(solution)/shard_map/ppermute | solution.py:12
  177.5 122.5 %all-reduce.3.cloned.1.call-start = ((), (), s32[]{:S(2)}) async-start(), calls=%async_computation | async-start | bytes 262144 | tf_op jit(solution)/shard_map/psum | solution.py:105
Sparse Core Ops, SparseCore 0:
  177.6 102.4 all-reduce.4
  283.0 16.9 all-reduce.2
where the time goes:
time: 310 us; the launch traced here: 308 us
  waiting for transfers between devices  142 us (46%)
  matrix products  56 us (18%)
  loops' own time  39.5 us (13%)
  local copies, waits for them, and re-layouts  31 us (10%)
  starting transfers between devices  23.6 us (8%)
  between operations  14.2 us (5%)
    psum x1, waiting for transfers between devices, on_device(): weight_grad = lax.psum(weight_terms, 'blk') * total_points ** (-0.5)  97.4 us
    another operation x1, loops' own time, point_block(): lax.scan(per_edge, (window_acc, start_total), edge_order)  39.5 us
    dot_general x20, matrix products, per_edge(): jnp.dot(picked, w_nbr_t, preferred_element_type=jnp.float32)  26.6 us
    ppermute x16, waiting for transfers between devices, shifted(): return lax.ppermute(block, axis, route)  26.1 us
    dot_general x20, matrix products, per_edge(): lax.dot_general(one_hot, edge_grad, (((0,), (0,)), ((), ())), preferred_e...  25.4 us
    ppermute x16, starting transfers between devices, shifted(): return lax.ppermute(block, axis, route)  23.5 us
    psum x1, waiting for transfers between devices, on_device(): feature_grad = lax.psum(summed, 'ch')  18.2 us
    dynamic_slice x20, local copies, waits for them, and re-layouts, per_edge(): slot_col = lax.dynamic_slice_in_dim(slot_rows, edge_index, 1, 1)  14.1 us
  transfers between devices with their start and end apart: 18, of which 9 were waited for; matrix products, arithmetic and copies ran while one was open for 3% of the time, Pallas kernels for 0%

commit v1 on v0

--- a/solution.py
+++ b/solution.py
@@ -96,7 +96,7 @@
     )
     weight_terms = jnp.concatenate([own_part, nbr_total - own_part], axis=1)
     total_points = points * lax.axis_size("blk")
-    weight_grad = lax.psum(weight_terms, "blk") * total_points ** (-0.5)
+    weight_grad = jnp.sum(lax.all_gather(weight_terms, "blk"), axis=0) * total_points ** (-0.5)
     self_grad = jnp.dot(grad_sum, w_diff, preferred_element_type=jnp.float32)
     contrib = jnp.dot(gathered, w_nbr, preferred_element_type=jnp.float32)
     contrib = contrib.reshape(2 * REACH + 1, points, in_width)

time: 310 us -> 231 us (0.75)
  waiting for transfers between devices: 142 us -> 60.2 us
    psum x1 -> x0, waiting for transfers between devices: 97.4 us -> none  [on_device(): weight_grad = lax.psum(weight_terms, 'blk') * total_points ** (-0.5)]
    all_gather x0 -> x1, waiting for transfers between devices: none -> 44 us  [on_device(): lax.all_gather(weight_terms, 'blk')]
    psum x1, waiting for transfers between devices: 18.2 us -> 0.01 us  [on_device(): feature_grad = lax.psum(summed, 'ch')]
    ppermute x16, waiting for transfers between devices: 26.1 us -> 16.2 us  [shifted(): return lax.ppermute(block, axis, route)]
  transfers between devices with their start and end apart: 18 -> 18, of which waited for: 9 -> 8; matrix products, arithmetic and copies ran while one was open for 3% -> 3% of each run, Pallas kernels for 0% -> 0%
where the time goes in v1:
time: 231 us; the launch traced here: 229 us
  waiting for transfers between devices  60.2 us (26%)
  matrix products  54.7 us (24%)
  loops' own time  39.5 us (17%)
  local copies, waits for them, and re-layouts  31.4 us (14%)
  starting transfers between devices  25.2 us (11%)
  between operations  15.7 us (7%)
    all_gather x1, waiting for transfers between devices, on_device(): lax.all_gather(weight_terms, 'blk')  44 us
    another operation x1, loops' own time, point_block(): lax.scan(per_edge, (window_acc, start_total), edge_order)  39.5 us
    dot_general x20, matrix products, per_edge(): jnp.dot(picked, w_nbr_t, preferred_element_type=jnp.float32)  26.6 us
    dot_general x20, matrix products, per_edge(): lax.dot_general(one_hot, edge_grad, (((0,), (0,)), ((), ())), preferred_e...  25.4 us
    ppermute x16, starting transfers between devices, shifted(): return lax.ppermute(block, axis, route)  25.1 us
    ppermute x16, waiting for transfers between devices, shifted(): return lax.ppermute(block, axis, route)  16.2 us
    dynamic_slice x20, local copies, waits for them, and re-layouts, per_edge(): slot_col = lax.dynamic_slice_in_dim(slot_rows, edge_index, 1, 1)  14.1 us
    dynamic_slice x20, local copies, waits for them, and re-layouts, point_block(): lax.scan(per_edge, (window_acc, start_total), edge_order)  11.7 us
  transfers between devices with their start and end apart: 18, of which 8 were waited for; matrix products, arithmetic and copies ran while one was open for 3% of the time, Pallas kernels for 0%

profile of v1, /device:TPU:0, one launch (start us, length us, event | category | flops | bytes accessed | tf_op | source)
XLA Modules:
  0.0 228.7 jit_solution(6072720790514264453)
XLA Ops:
  8.1 3.1 %collective-permute-start = (bf16[256,128]{1,0:T(8,128)(2,1)}, bf16[256,128]{1,0:T(8,128)(2,1)S(1)}, u32[]{:S(2)}, u32[]{:S(2)}) collective-permute-start(bf16[256,128]{1,0:T(8,128)(2,1)} %param.9), channel_id=1, source_target_pairs={{24,0},{26,2},{28,4},{30,6},{0,8},{2,10},{4,12},{6,14},{8,16},{10,... | collective-permute-start | bytes 196616 | tf_op jit(solution)/shard_map/ppermute | solution.py:12
  11.2 2.4 %collective-permute-start.1 = (bf16[256,128]{1,0:T(8,128)(2,1)}, bf16[256,128]{1,0:T(8,128)(2,1)S(1)}, u32[]{:S(2)}, u32[]{:S(2)}) collective-permute-start(bf16[256,128]{1,0:T(8,128)(2,1)} %param.9), channel_id=1, source_target_pairs={{26,0},{28,2},{30,4},{0,6},{2,8},{4,10},{6,12},{8,14},{10,16},{12,... | collective-permute-start | bytes 196616 | tf_op jit(solution)/shard_map/ppermute | solution.py:12
  13.6 1.5 collective-permute-start.2
  15.7 5.0 %collective-permute-start.4 = (bf16[256,128]{1,0:T(8,128)(2,1)}, bf16[256,128]{1,0:T(8,128)(2,1)S(1)}, u32[]{:S(2)}, u32[]{:S(2)}) collective-permute-start(bf16[256,128]{1,0:T(8,128)(2,1)} %param.9), channel_id=1, source_target_pairs={{2,0},{4,2},{6,4},{8,6},{10,8},{12,10},{14,12},{16,14},{18,16},{20... | collective-permute-start | bytes 196616 | tf_op jit(solution)/shard_map/ppermute | solution.py:12
  25.4 2.9 %collective-permute-done.5 = bf16[256,128]{1,0:T(8,128)(2,1)S(1)} collective-permute-done((bf16[256,128]{1,0:T(8,128)(2,1)}, bf16[256,128]{1,0:T(8,128)(2,1)S(1)}, u32[]{:S(2)}, u32[]{:S(2)}) %collective-permute-start.5) | collective-permute-done | bytes 65568 | tf_op jit(solution)/shard_map/ppermute | solution.py:12
  28.4 1.5 collective-permute-done.6
  29.9 117.3 %while.23 = (s32[]{:T(128)}, f32[2304,128]{1,0:T(8,128)S(1)}, f32[256,128]{1,0:T(8,128)S(1)}, s32[20]{0:T(128)S(1)}, s32[256,20]{0,1:T(8,128)}, /*index=5*/s32[2...) while((s32[]{:T(128)}, f32[2304,128]{1,0:T(8,128)S(1)}, ...), condition=%wide.region_1.2_spmd.clone, body=%wide.region_0.1_spmd.clone.sunk | while | flops 312672256 | bytes 3772606 | solution.py:75
  33.1 1.3 select_add_fusion.2
  39.0 1.3 select_add_fusion.2
  44.8 1.3 select_add_fusion.2
  50.7 1.3 select_add_fusion.2
  62.4 1.3 select_add_fusion.2
  68.3 1.3 select_add_fusion.2
  80.0 1.3 select_add_fusion.2
  85.9 1.3 select_add_fusion.2
  97.6 1.3 select_add_fusion.2
  103.5 1.3 select_add_fusion.2
  115.2 1.3 select_add_fusion.2
  121.1 1.3 select_add_fusion.2
  126.9 1.3 select_add_fusion.2
  132.8 1.3 select_add_fusion.2
  138.7 1.3 select_add_fusion.2
  144.5 1.3 select_add_fusion.2
  148.9 4.1 %collective-permute-start.10 = (f32[256,128]{1,0:T(8,128)S(1)}, f32[256,128]{1,0:T(8,128)S(1)}, u32[]{:S(2)}, u32[]{:S(2)}) collective-permute-start(f32[256,128]{1,0:T(8,128)S(1)} %get-tuple-element.192), channel_id=1, source_target_pairs={{4,0},{6,2},{8,4},{10,6},{12,8},{14,10},{16,12},{18,14},{20,16},{2... | collective-permute-start | bytes 393224 | tf_op jit(solution)/shard_map/ppermute | solution.py:12
  155.1 1.6 collective-permute-start.14
  157.6 1.8 collective-permute-done.11
  159.4 2.3 collective-permute-start.8
  161.7 3.3 %collective-permute-done.12 = f32[256,128]{1,0:T(8,128)S(1)} collective-permute-done((f32[256,128]{1,0:T(8,128)S(1)}, f32[256,128]{1,0:T(8,128)S(1)}, u32[]{:S(2)}, u32[]{:S(2)}) %collective-permute-start.12) | collective-permute-done | bytes 131104 | tf_op jit(solution)/shard_map/ppermute | solution.py:12
  166.4 5.2 %collective-permute-done.9 = f32[256,128]{1,0:T(8,128)S(1)} collective-permute-done((f32[256,128]{1,0:T(8,128)S(1)}, f32[256,128]{1,0:T(8,128)S(1)}, u32[]{:S(2)}, u32[]{:S(2)}) %collective-permute-start.9) | collective-permute-done | bytes 131104 | tf_op jit(solution)/shard_map/ppermute | solution.py:12
  172.5 44.0 %all-gather.3.cloned.1.call-done = f32[2048,256]{0,1:T(8,128)} async-done(((f32[128,256]{0,1:T(8,128)}), f32[2048,256]{0,1:T(8,128)}) %all-gather.3.cloned.1.call-update) | async-done | bytes 2097168 | tf_op jit(solution)/shard_map/all_gather | solution.py:99
  216.6 2.0 copy.16
  219.7 1.6 copy.35
  (122 shorter events, 69.9 us)
Async XLA Ops:
  8.0 16.5 %copy-start = (bf16[256,128]{1,0:T(8,128)(2,1)S(1)}, bf16[256,128]{1,0:T(8,128)(2,1)}, u32[]{:S(2)}) copy-start(bf16[256,128]{1,0:T(8,128)(2,1)} %param.9) | copy-start | bytes 196612
  8.0 21.9 %copy-start.2 = (s32[256,128]{1,0:T(8,128)S(1)}, s32[256,128]{1,0:T(8,128)}, u32[]{:S(2)}) copy-start(s32[256,128]{1,0:T(8,128)} %param.13) | copy-start | bytes 393220
  8.0 208.5 %all-gather.3.cloned.1.call-start = ((), (), s32[]{:S(2)}) async-start(), calls=%async_computation.1 | async-start | bytes 2228224 | tf_op jit(solution)/shard_map/all_gather | solution.py:99
  8.1 15.7 %collective-permute-start = (bf16[256,128]{1,0:T(8,128)(2,1)}, bf16[256,128]{1,0:T(8,128)(2,1)S(1)}, u32[]{:S(2)}, u32[]{:S(2)}) collective-permute-start(bf16[256,128]{1,0:T(8,128)(2,1)} %param.9), channel_id=1, source_target_pairs={{24,0},{26,2},{28,4},{30,6},{0,8},{2,10},{4,12},{6,14},{8,16},{10,... | collective-permute-start | bytes 196616 | tf_op jit(solution)/shard_map/ppermute | solution.py:12
  11.2 13.2 %collective-permute-start.1 = (bf16[256,128]{1,0:T(8,128)(2,1)}, bf16[256,128]{1,0:T(8,128)(2,1)S(1)}, u32[]{:S(2)}, u32[]{:S(2)}) collective-permute-start(bf16[256,128]{1,0:T(8,128)(2,1)} %param.9), channel_id=1, source_target_pairs={{26,0},{28,2},{30,4},{0,6},{2,8},{4,10},{6,12},{8,14},{10,16},{12,... | collective-permute-start | bytes 196616 | tf_op jit(solution)/shard_map/ppermute | solution.py:12
  13.6 10.9 %collective-permute-start.2 = (bf16[256,128]{1,0:T(8,128)(2,1)}, bf16[256,128]{1,0:T(8,128)(2,1)S(1)}, u32[]{:S(2)}, u32[]{:S(2)}) collective-permute-start(bf16[256,128]{1,0:T(8,128)(2,1)} %param.9), channel_id=1, source_target_pairs={{28,0},{30,2},{0,4},{2,6},{4,8},{6,10},{8,12},{10,14},{12,16},{14,... | collective-permute-start | bytes 196616 | tf_op jit(solution)/shard_map/ppermute | solution.py:12
  15.1 10.2 %collective-permute-start.3 = (bf16[256,128]{1,0:T(8,128)(2,1)}, bf16[256,128]{1,0:T(8,128)(2,1)S(1)}, u32[]{:S(2)}, u32[]{:S(2)}) collective-permute-start(bf16[256,128]{1,0:T(8,128)(2,1)} %param.9), channel_id=1, source_target_pairs={{30,0},{0,2},{2,4},{4,6},{6,8},{8,10},{10,12},{12,14},{14,16},{16,... | collective-permute-start | bytes 196616 | tf_op jit(solution)/shard_map/ppermute | solution.py:12
  15.7 9.6 %collective-permute-start.4 = (bf16[256,128]{1,0:T(8,128)(2,1)}, bf16[256,128]{1,0:T(8,128)(2,1)S(1)}, u32[]{:S(2)}, u32[]{:S(2)}) collective-permute-start(bf16[256,128]{1,0:T(8,128)(2,1)} %param.9), channel_id=1, source_target_pairs={{2,0},{4,2},{6,4},{8,6},{10,8},{12,10},{14,12},{16,14},{18,16},{20... | collective-permute-start | bytes 196616 | tf_op jit(solution)/shard_map/ppermute | solution.py:12
  23.8 4.5 %collective-permute-start.5 = (bf16[256,128]{1,0:T(8,128)(2,1)}, bf16[256,128]{1,0:T(8,128)(2,1)S(1)}, u32[]{:S(2)}, u32[]{:S(2)}) collective-permute-start(bf16[256,128]{1,0:T(8,128)(2,1)} %param.9), channel_id=1, source_target_pairs={{4,0},{6,2},{8,4},{10,6},{12,8},{14,10},{16,12},{18,14},{20,16},{2... | collective-permute-start | bytes 196616 | tf_op jit(solution)/shard_map/ppermute | solution.py:12
  24.4 5.4 %collective-permute-start.6 = (bf16[256,128]{1,0:T(8,128)(2,1)}, bf16[256,128]{1,0:T(8,128)(2,1)S(1)}, u32[]{:S(2)}, u32[]{:S(2)}) collective-permute-start(bf16[256,128]{1,0:T(8,128)(2,1)} %param.9), channel_id=1, source_target_pairs={{6,0},{8,2},{10,4},{12,6},{14,8},{16,10},{18,12},{20,14},{22,16},{... | collective-permute-start | bytes 196616 | tf_op jit(solution)/shard_map/ppermute | solution.py:12
  24.5 5.3 %collective-permute-start.7 = (bf16[256,128]{1,0:T(8,128)(2,1)S(1)}, bf16[256,128]{1,0:T(8,128)(2,1)S(1)}, u32[]{:S(2)}, u32[]{:S(2)}) collective-permute-start(bf16[256,128]{1,0:T(8,128)(2,1)S(1)} %copy-done), channel_id=1, source_target_pairs={{8,0},{10,2},{12,4},{14,6},{16,8},{18,10},{20,12},{22,14},{24,16},... | collective-permute-start | bytes 196616 | tf_op jit(solution)/shard_map/ppermute | solution.py:12
  147.4 1.1 copy-start.1
  148.4 71.2 %all-reduce.2.cloned.1.call-start = ((), (), s32[]{:S(2)}) async-start(), calls=%async_computation | async-start | bytes 262144 | tf_op jit(solution)/shard_map/psum | solution.py:105
  148.9 7.8 %collective-permute-start.10 = (f32[256,128]{1,0:T(8,128)S(1)}, f32[256,128]{1,0:T(8,128)S(1)}, u32[]{:S(2)}, u32[]{:S(2)}) collective-permute-start(f32[256,128]{1,0:T(8,128)S(1)} %get-tuple-element.192), channel_id=1, source_target_pairs={{4,0},{6,2},{8,4},{10,6},{12,8},{14,10},{16,12},{18,14},{20,16},{2... | collective-permute-start | bytes 393224 | tf_op jit(solution)/shard_map/ppermute | solution.py:12
  153.0 6.4 %collective-permute-start.11 = (f32[256,128]{1,0:T(8,128)S(1)}, f32[256,128]{1,0:T(8,128)S(1)}, u32[]{:S(2)}, u32[]{:S(2)}) collective-permute-start(f32[256,128]{1,0:T(8,128)S(1)} %get-tuple-element.191), channel_id=1, source_target_pairs={{2,0},{4,2},{6,4},{8,6},{10,8},{12,10},{14,12},{16,14},{18,16},{20... | collective-permute-start | bytes 393224 | tf_op jit(solution)/shard_map/ppermute | solution.py:12
  154.3 10.7 %collective-permute-start.12 = (f32[256,128]{1,0:T(8,128)S(1)}, f32[256,128]{1,0:T(8,128)S(1)}, u32[]{:S(2)}, u32[]{:S(2)}) collective-permute-start(f32[256,128]{1,0:T(8,128)S(1)} %get-tuple-element.190), channel_id=1, source_target_pairs={{30,0},{0,2},{2,4},{4,6},{6,8},{8,10},{10,12},{12,14},{14,16},{16,... | collective-permute-start | bytes 393224 | tf_op jit(solution)/shard_map/ppermute | solution.py:12
  155.1 9.9 %collective-permute-start.13 = (f32[256,128]{1,0:T(8,128)S(1)}, f32[256,128]{1,0:T(8,128)S(1)}, u32[]{:S(2)}, u32[]{:S(2)}) collective-permute-start(f32[256,128]{1,0:T(8,128)S(1)} %get-tuple-element.189), channel_id=1, source_target_pairs={{28,0},{30,2},{0,4},{2,6},{4,8},{6,10},{8,12},{10,14},{12,16},{14,... | collective-permute-start | bytes 393224 | tf_op jit(solution)/shard_map/ppermute | solution.py:12
  155.1 10.4 %collective-permute-start.14 = (f32[256,128]{1,0:T(8,128)S(1)}, f32[256,128]{1,0:T(8,128)S(1)}, u32[]{:S(2)}, u32[]{:S(2)}) collective-permute-start(f32[256,128]{1,0:T(8,128)S(1)} %get-tuple-element.188), channel_id=1, source_target_pairs={{26,0},{28,2},{30,4},{0,6},{2,8},{4,10},{6,12},{8,14},{10,16},{12,... | collective-permute-start | bytes 393224 | tf_op jit(solution)/shard_map/ppermute | solution.py:12
  156.7 8.8 %collective-permute-start.15 = (f32[256,128]{1,0:T(8,128)S(1)}, f32[256,128]{1,0:T(8,128)S(1)}, u32[]{:S(2)}, u32[]{:S(2)}) collective-permute-start(f32[256,128]{1,0:T(8,128)S(1)} %get-tuple-element.187), channel_id=1, source_target_pairs={{24,0},{26,2},{28,4},{30,6},{0,8},{2,10},{4,12},{6,14},{8,16},{10,... | collective-permute-start | bytes 393224 | tf_op jit(solution)/shard_map/ppermute | solution.py:12
  159.4 7.0 %collective-permute-start.8 = (f32[256,128]{1,0:T(8,128)S(1)}, f32[256,128]{1,0:T(8,128)S(1)}, u32[]{:S(2)}, u32[]{:S(2)}) collective-permute-start(f32[256,128]{1,0:T(8,128)S(1)} %get-tuple-element.186), channel_id=1, source_target_pairs={{8,0},{10,2},{12,4},{14,6},{16,8},{18,10},{20,12},{22,14},{24,16},... | collective-permute-start | bytes 393224 | tf_op jit(solution)/shard_map/ppermute | solution.py:12
  165.0 6.7 %collective-permute-start.9 = (f32[256,128]{1,0:T(8,128)S(1)}, f32[256,128]{1,0:T(8,128)S(1)}, u32[]{:S(2)}, u32[]{:S(2)}) collective-permute-start(f32[256,128]{1,0:T(8,128)S(1)} %get-tuple-element.193), channel_id=1, source_target_pairs={{6,0},{8,2},{10,4},{12,6},{14,8},{16,10},{18,12},{20,14},{22,16},{... | collective-permute-start | bytes 393224 | tf_op jit(solution)/shard_map/ppermute | solution.py:12
Sparse Core Ops, SparseCore 0:
  148.6 67.9 all-gather.2
Sparse Core Ops, SparseCore 1:
  172.6 16.7 all-reduce.1
